TPU v7x, 32 devices: a whole 2x2x4 slice. The times are simulated.
32 devices in a mesh: task: 4 (over x, core), dp: 8 (over z, y).
Axes of the slice: x: 2, y: 2, z: 4, core: 2. Of those that a mesh axis runs over, the one named last changes fastest.
Arguments:
- inputs: bfloat16 [8192, 4096], P('dp'), may hold values from -6 to 6
- cotangent: bfloat16 [4, 8192, 1024], P('task', 'dp'), may hold values from -0.44194174 to 0.44194174
- task_order: int32 [4], replicated, may hold values from 0 to 3, each once
- conflict_flags: int32 [4, 4], replicated, may hold values 0 or 1
Outputs:
- combined: bfloat16 [4096, 1024], P(None, 'task')
Inputs may be any that keep to these rules, and one draw needn't show every extreme that they name: `task_order`: a permutation of the tasks. `conflict_flags`: diagonal entries are ignored.
All inputs are finite; a program needn't handle non-finite values.
Results may differ from a plain program's by a relative error of at most 0.001.
Values may be sent and summed in bfloat16 or wider, within the bound.
A program may use at most 128 MiB of HBM per device.

v0:
```python
import jax
import jax.numpy as jnp
from jax import lax
from jax.sharding import PartitionSpec as P


def project_weights(gram_matrix, task_order, conflict_flags):
    count = gram_matrix.shape[0]
    labels = jnp.arange(count, dtype=jnp.int32)
    coefficients = jnp.eye(count, dtype=jnp.float32)
    for position in range(count):
        target = task_order[position]
        pick_column = (labels == target).astype(jnp.float32)
        column = jnp.dot(gram_matrix, pick_column, precision=lax.Precision.HIGHEST)
        inner_dots = jnp.dot(coefficients, column, precision=lax.Precision.HIGHEST)
        own_square = jnp.sum(pick_column * column)
        active = jnp.dot(
            conflict_flags.astype(jnp.float32), pick_column, precision=lax.Precision.HIGHEST
        ) * (1.0 - pick_column)
        removed = jnp.minimum(inner_dots, 0.0) / own_square * active
        coefficients = coefficients - removed[:, None] * pick_column[None, :]
    return jnp.sum(coefficients, axis=0)


def on_device(inputs, cotangent, task_order, conflict_flags):
    task_cot = cotangent[0]
    shard_grad = lax.psum_scatter(
        lax.dot_general(
            inputs, task_cot, (((0,), (0,)), ((), ())), preferred_element_type=jnp.float32
        ),
        "dp",
        scatter_dimension=0,
        tiled=True,
    )
    own_grads = lax.all_to_all(shard_grad[None], "task", split_axis=2, concat_axis=0, tiled=True)
    gram_part = jnp.einsum("tab,sab->ts", own_grads, own_grads, precision=lax.Precision.HIGHEST)
    gram_matrix = lax.psum(gram_part, ("task", "dp"))
    weights = project_weights(gram_matrix, task_order, conflict_flags)
    own_block = jnp.einsum("t,tab->ab", weights, own_grads, precision=lax.Precision.HIGHEST)
    return lax.all_gather(own_block.astype(jnp.bfloat16), "dp", axis=0, tiled=True)


def solution(mesh):
    in_specs = (P("dp", None), P("task", "dp", None), P(), P())
    out_specs = P(None, "task")
    return jax.shard_map(
        on_device, mesh=mesh, in_specs=in_specs, out_specs=out_specs, check_vma=False
    )
```

profile of v0, /device:TPU:0, one launch (start us, length us, event | category | flops | bytes accessed | tf_op | source)
XLA Modules:
  0.0 474.5 jit_solution(15672404880524209670)
XLA Ops:
  6.5 0.0 copy-start
  6.5 0.0 reduce-scatter.2.cloned.1.call-start
  6.5 1.6 copy-done
  8.1 14.6 %fusion.4 = f32[4096,1024]{1,0:T(8,128)} fusion(bf16[1024,4096]{1,0:T(8,128)(2,1)} %param.4, bf16[1,1024,1024]{2,1,0:T(8,128)(2,1)S(1)} %copy-done), kind=kOutput, calls=%fused_computation.4 | convolution fusion | flops 8589934592 | bytes 27262976 | tf_op jit(solution)/shard_map/dot_general | solution.py:28
  22.7 0.0 reduce-scatter.2.cloned.1.call-update
  22.7 282.3 %reduce-scatter.2.cloned.1.call-done = f32[512,1024]{1,0:T(8,128)} async-done(((f32[4096,1024]{1,0:T(8,128)}), f32[512,1024]{1,0:T(8,128)}) %reduce-scatter.2.cloned.1.call-update) | async-done | bytes 2097168 | tf_op jit(solution)/shard_map/reduce_scatter | solution.py:27
  305.1 6.0 %copy.7 = f32[1,512,1024]{1,0,2:T(1,128)} copy(f32[1,512,1024]{2,1,0:T(8,128)} %bitcast.140) | data formatting | bytes 4194304 | tf_op jit(solution)/shard_map/broadcast_in_dim | solution.py:35
  311.1 0.0 copy-start.1
  311.1 0.0 copy-start.2
  311.1 4.6 all-to-all-start
  315.7 0.2 all-gather.2.cloned.1.call-start
  315.9 0.0 copy-done.1
  315.9 0.6 fusion.74
  316.5 1.2 fusion.61
  317.8 0.0 copy-done.2
  317.8 0.7 fusion.22
  318.5 0.7 fusion.18
  319.2 0.7 fusion.14
  319.9 21.5 %all-to-all-done = f32[1,512,1024]{1,0,2:T(1,128)} async-done(((f32[1,512,1024]{1,0,2:T(1,128)}), f32[1,512,1024]{1,0,2:T(1,128)}, u32[]{:S(2)}, u32[]{:S(2)}) %all-to-all-start) | async-done | bytes 2097184 | tf_op jit(solution)/shard_map/all_to_all | solution.py:35
  341.4 3.1 copy.11
  344.5 2.9 copy.10
  347.4 12.0 %fusion.6 = f32[4,4]{1,0:T(4,128)S(1)} fusion(f32[1,512,4,256]{3,2,1,0:T(4,128)} %copy.10), kind=kOutput, calls=%fused_computation.6 | convolution fusion | flops 25165824 | bytes 2097216 | tf_op jit(solution)/shard_map/tab,sab->ts/dot_general | solution.py:36
  359.4 1.2 fusion.63
  360.6 38.6 %psum.7 = f32[4,4]{1,0:T(4,128)S(1)} all-reduce(f32[4,4]{1,0:T(4,128)S(1)} %fusion.6), channel_id=1, replica_groups=mesh['task'=4,'dp'=8] {'task','dp'}, use_global_device_ids=true, to_apply=%region_1.0 | all-reduce | flops 16 | bytes 128 | tf_op jit(solution)/shard_map/psum | solution.py:37
  399.2 1.3 fusion.60
  400.5 1.3 fusion.59
  401.8 1.3 fusion.57
  403.2 1.3 fusion.55
  404.5 0.8 fusion.24
  405.3 0.7 fusion.10
  406.0 0.8 fusion.13
  406.8 0.8 fusion.17
  407.6 0.8 fusion.21
  408.4 0.1 subtract_reduce_fusion
  408.5 5.4 %fusion = bf16[1,512,256]{2,0,1:T(2,128)(2,1)S(1)} fusion(f32[1,512,4,256]{3,2,1,0:T(4,128)} %copy.10, f32[4]{0:T(128)S(1)} %subtract_reduce_fusion), kind=kOutput, calls=%fused_computation | convolution fusion | flops 6291456 | bytes 2359312 | tf_op jit(solution)/shard_map/t,tab->ab/dot_general | solution.py:39
  413.9 0.7 copy.13
  414.7 0.0 all-gather.2.cloned.1.call-update
  414.7 49.9 %all-gather.2.cloned.1.call-done = bf16[4096,256]{1,0:T(8,128)(2,1)} async-done(((bf16[512,256]{1,0:T(8,128)(2,1)}), bf16[4096,256]{1,0:T(8,128)(2,1)}) %all-gather.2.cloned.1.call-update) | async-done | bytes 2097168 | tf_op jit(solution)/shard_map/all_gather | solution.py:40
  464.6 3.0 copy.15
Async XLA Ops:
  6.5 1.6 copy-start
  6.5 298.5 %reduce-scatter.2.cloned.1.call-start = ((), (), s32[]{:S(2)}) async-start(), calls=%async_computation.2 | async-start | bytes 18874368 | tf_op jit(solution)/shard_map/reduce_scatter | solution.py:27
  311.1 4.8 %copy-start.1 = (s32[4]{0:T(128)S(1)}, s32[4]{0:T(128)}, u32[]{:S(2)}) copy-start(s32[4]{0:T(128)} %param.6) | copy-start | bytes 52
  311.1 6.7 %copy-start.2 = (s32[4,4]{1,0:T(4,128)S(1)}, s32[4,4]{1,0:T(4,128)}, u32[]{:S(2)}) copy-start(s32[4,4]{1,0:T(4,128)} %param.7) | copy-start | bytes 196
  311.1 30.3 %all-to-all-start = ((f32[1,512,1024]{1,0,2:T(1,128)}), f32[1,512,1024]{1,0,2:T(1,128)}, u32[]{:S(2)}, u32[]{:S(2)}) async-start(f32[1,512,1024]{1,0,2:T(1,128)} %copy.7), calls=%async_computation.1 | async-start | bytes 4194304 | tf_op jit(solution)/shard_map/all_to_all | solution.py:35
  315.7 149.0 %all-gather.2.cloned.1.call-start = ((), (), s32[]{:S(2)}) async-start(), calls=%async_computation.3 | async-start | bytes 2359296 | tf_op jit(solution)/shard_map/all_gather | solution.py:40
Sparse Core Ops, SparseCore 0:
  22.8 282.1 reduce-scatter.1
  414.8 49.7 all-gather.1
where the time goes:
time: 475 us
  waiting for transfers between devices  354 us (75%)
  matrix products  43.3 us (9%)
  blocking collectives  38.6 us (8%)
  local copies, waits for them, and re-layouts  18.1 us (4%)
  between operations  13.5 us (3%)
  starting transfers between devices  4.8 us (1%)
    reduce_scatter x1, waiting for transfers between devices, on_device(): lax.psum_scatter(lax.dot_general(inputs, task_cot, (((0,), (0,)), ((), ()...  282 us
    all_gather x1, waiting for transfers between devices, on_device(): lax.all_gather(own_block.astype(jnp.bfloat16), 'dp', axis=0, tiled=True)  49.9 us
    psum x1, blocking collectives, on_device(): gram_matrix = lax.psum(gram_part, ('task', 'dp'))  38.6 us
    all_to_all x1, waiting for transfers between devices, on_device(): lax.all_to_all(shard_grad[None], 'task', split_axis=2, concat_axis=0, til...  21.5 us
    dot_general x1, matrix products, on_device(): lax.dot_general(inputs, task_cot, (((0,), (0,)), ((), ())), preferred_ele...  14.6 us
    dot_general x1, matrix products, on_device(): jnp.einsum('tab,sab->ts', own_grads, own_grads, precision=lax.Precision.H...  12 us
  transfers between devices with their start and end apart: 3, of which 3 were waited for; matrix products, arithmetic and copies ran while one was open for 1% of the time, Pallas kernels for 0%

commit v1 on v0

v1 whole, which is shorter than its diff:
```python
import functools

import jax
import jax.numpy as jnp
from jax import lax
from jax.experimental import pallas as pl
from jax.experimental.pallas import tpu as pltpu
from jax.sharding import PartitionSpec as P

MESH = pl.DeviceIdType.MESH
TOP = 32767.0


def coded(tile):
    high = jnp.maximum(jnp.max(jnp.abs(tile), axis=0, keepdims=True), 1e-30)
    code = jnp.round(tile * (TOP / high)).astype(jnp.int32).astype(jnp.int16)
    return code, high * (1.0 / TOP)


def decoded(code, scale):
    return code.astype(jnp.int32).astype(jnp.float32) * scale


def kernel(tasks, ndp, chunks, order_ref, flags_ref, x_ref, c_ref, out_ref,
           ysend, yscale, yrecv, yrscale, zsend, zscale, zrecv, zrscale, own,
           gsend, grads, gram_own, gram_dp, gram_mid, gram_task,
           ys_sem, yr_sem, zs_sem, zr_sem, ts_sem, tr_sem, gs_sem, gr_sem,
           hs_sem, hr_sem, as_sem, ar_sem):
    nz = ndp // 2
    me_t = lax.axis_index("task")
    me_d = lax.axis_index("dp")
    z = me_d // 2
    y = me_d % 2
    rows = x_ref.shape[1] // ndp
    step = rows // chunks
    width = c_ref.shape[1] // tasks

    def zof(k):
        return lax.rem(z + k, nz)

    def dp_at(zi, yi):
        return zi * 2 + yi

    partner = (me_t, dp_at(z, 1 - y))

    barrier = pltpu.get_barrier_semaphore()
    for k in range(1, ndp):
        pl.semaphore_signal(barrier, inc=1, device_id=(me_t, lax.rem(me_d + k, ndp)), device_id_type=MESH)
    for k in range(1, tasks):
        pl.semaphore_signal(barrier, inc=1, device_id=(lax.rem(me_t + k, tasks), me_d), device_id_type=MESH)
    pl.semaphore_wait(barrier, ndp + tasks - 2)

    def send(src, dst, s, r, device):
        copy = pltpu.make_async_remote_copy(src_ref=src, dst_ref=dst, send_sem=s, recv_sem=r,
                                            device_id=device, device_id_type=MESH)
        copy.start()
        return copy

    def product(zi, yi, c):
        first = pl.multiple_of(dp_at(zi, yi) * rows + c * step, step)
        return lax.dot_general(x_ref[:, pl.ds(first, step)], c_ref[...], (((0,), (0,)), ((), ())),
                               preferred_element_type=jnp.float32)

    ycopies, zcopies, tcopies = {}, {}, {}
    for c in range(chunks):
        def fill(k, carry, c=c):
            code, scale = coded(product(zof(k), 1 - y, c))
            ysend[c, k] = code
            yscale[c, k] = scale
            return carry
        lax.fori_loop(0, nz, fill, 0)
        ycopies[c] = (send(ysend.at[c], yrecv.at[c], ys_sem.at[c, 0], yr_sem.at[c, 0], partner),
                      send(yscale.at[c], yrscale.at[c], ys_sem.at[c, 1], yr_sem.at[c, 1], partner))

    def second(c):
        for copy in ycopies[c]:
            copy.wait_recv()
        zcopies[c] = []
        for k in [*range(nz - 1, 0, -1), 0]:
            total = product(zof(k), y, c) + decoded(yrecv[c, k], yrscale[c, k])
            if k == 0:
                own[c] = total
            else:
                code, scale = coded(total)
                zsend[c, k] = code
                zscale[c, k] = scale
                peer = (me_t, dp_at(zof(k), y))
                zcopies[c] += [send(zsend.at[c, k], zrecv.at[c, k], zs_sem.at[c, k, 0], zr_sem.at[c, k, 0], peer),
                               send(zscale.at[c, k], zrscale.at[c, k], zs_sem.at[c, k, 1], zr_sem.at[c, k, 1], peer)]

    def third(c):
        for copy in zcopies[c]:
            copy.wait_recv()
        total = own[c]
        for k in range(1, nz):
            total = total + decoded(zrecv[c, k], zrscale[c, k])
        for t in range(tasks):
            gsend[c, t] = total[:, t * width:(t + 1) * width]
        grads[me_t, c] = gsend[c, me_t]
        tcopies[c] = []
        for k in range(1, tasks):
            peer = lax.rem(me_t + k, tasks)
            tcopies[c].append(send(gsend.at[c, peer], grads.at[me_t, c], ts_sem.at[c, k], tr_sem.at[c, k],
                                   (peer, me_d)))

    second(0)
    for c in range(1, chunks):
        second(c)
        third(c - 1)
    third(chunks - 1)

    line = lax.broadcasted_iota(jnp.int32, (8, 128), 0)
    lane = lax.broadcasted_iota(jnp.int32, (8, 128), 1)
    gram = jnp.zeros((8, 128), jnp.float32)
    for c in range(chunks):
        for copy in tcopies[c]:
            copy.wait_recv()
    for s in range(tasks):
        for t in range(s, tasks):
            def add(c, total, s=s, t=t):
                both = grads[s, c] * grads[t, c]
                return total + jnp.sum(both.reshape(step // 8, 8, width), axis=0)
            total = lax.fori_loop(0, chunks, add, jnp.zeros((8, width), jnp.float32))
            value = jnp.sum(jnp.sum(total, axis=0, keepdims=True), axis=1, keepdims=True)
            here = ((line == s) & (lane == t)) | ((line == t) & (lane == s))
            gram = gram + jnp.where(here, value, 0.0)

    def swap(value, buffer_own, buffer, count, s_sem, r_sem, device):
        buffer_own[...] = value
        copies = [send(buffer_own, buffer.at[k], s_sem.at[k], r_sem.at[k], device(k)) for k in range(1, count)]
        for k, copy in enumerate(copies, 1):
            copy.wait_recv()
            value = value + buffer[k]
        for copy in copies:
            copy.wait_send()
        return value

    gram = swap(gram, gram_own, gram_dp, ndp, gs_sem, gr_sem, lambda k: (me_t, lax.rem(me_d + k, ndp)))
    gram = swap(gram, gram_mid, gram_task, tasks, hs_sem, hr_sem, lambda k: (lax.rem(me_t + k, tasks), me_d))

    cols = [jnp.sum(jnp.where(lane == m, gram, 0.0), axis=1, keepdims=True) for m in range(tasks)]
    entry = lambda column, i: jnp.sum(jnp.where(line[:, :1] == i, column, 0.0), axis=0, keepdims=True)
    row = line[:, :1]
    coefficients = [(row == m).astype(jnp.float32) for m in range(tasks)]
    flag_cols = []
    for m in range(tasks):
        column = jnp.zeros((8, 1), jnp.float32)
        for i in range(tasks):
            column = column + jnp.where(row == i, flags_ref[i, m].astype(jnp.float32), 0.0)
        flag_cols.append(column)
    for position in range(tasks):
        target = order_ref[position]
        picks = [jnp.where(target == m, 1.0, 0.0) for m in range(tasks)]
        column = sum(cols[m] * picks[m] for m in range(tasks))
        dots = sum(coefficients[m] * entry(column, m) for m in range(tasks))
        square = sum(entry(column, m) * picks[m] for m in range(tasks))
        active = sum(flag_cols[m] * picks[m] for m in range(tasks)) * jnp.where(row == target, 0.0, 1.0)
        removed = jnp.minimum(dots, 0.0) / square * active
        coefficients = [coefficients[m] - removed * picks[m] for m in range(tasks)]
    weights = [jnp.sum(coefficients[m], axis=0, keepdims=True) for m in range(tasks)]

    def block(d):
        return out_ref.at[pl.ds(pl.multiple_of(d * rows, rows), rows), :]

    for c in range(chunks):
        mixed = sum(weights[t] * grads[t, c] for t in range(tasks))
        out_ref[pl.ds(pl.multiple_of(me_d * rows + c * step, step), step), :] = mixed.astype(jnp.bfloat16)
    mine = block(me_d)
    along = {k: send(mine, mine, as_sem.at[0, k], ar_sem.at[0, k], (me_t, dp_at(zof(k), y)))
             for k in range(1, nz)}
    across = [send(mine, mine, as_sem.at[1, 0], ar_sem.at[1, 0], partner)]
    for k in range(1, nz):
        along[k].wait_recv()
        held = block(dp_at(lax.rem(z + nz - k, nz), y))
        across.append(send(held, held, as_sem.at[1, k], ar_sem.at[1, k], partner))
    for copy in across:
        copy.wait_recv()
    for copy in [*across, *along.values()]:
        copy.wait_send()
    for group in (ycopies, zcopies, tcopies):
        for c in range(chunks):
            for copy in group[c]:
                copy.wait_send()


def solution(mesh):
    tasks, ndp = mesh.shape["task"], mesh.shape["dp"]
    nz = ndp // 2

    def on_device(inputs, cotangent, task_order, conflict_flags):
        cot = cotangent[0]
        rows = inputs.shape[1] // ndp
        step = min(rows, 128)
        chunks = rows // step
        kvw = cot.shape[1]
        width = kvw // tasks
        vmem, dma = pltpu.VMEM, pltpu.SemaphoreType.DMA
        f32, i16 = jnp.float32, jnp.int16
        scratch = [
            vmem((chunks, nz, step, kvw), i16), vmem((chunks, nz, 1, kvw), f32),
            vmem((chunks, nz, step, kvw), i16), vmem((chunks, nz, 1, kvw), f32),
            vmem((chunks, nz, step, kvw), i16), vmem((chunks, nz, 1, kvw), f32),
            vmem((chunks, nz, step, kvw), i16), vmem((chunks, nz, 1, kvw), f32),
            vmem((chunks, step, kvw), f32),
            vmem((chunks, tasks, step, width), f32), vmem((tasks, chunks, step, width), f32),
            vmem((8, 128), f32), vmem((ndp, 8, 128), f32), vmem((8, 128), f32), vmem((tasks, 8, 128), f32),
            dma((chunks, 2)), dma((chunks, 2)), dma((chunks, nz, 2)), dma((chunks, nz, 2)),
            dma((chunks, tasks)), dma((chunks, tasks)), dma((ndp,)), dma((ndp,)),
            dma((tasks,)), dma((tasks,)), dma((2, nz)), dma((2, nz)),
        ]
        smem = pl.BlockSpec(memory_space=pltpu.SMEM)
        whole = pl.BlockSpec(memory_space=pltpu.VMEM)
        return pl.pallas_call(
            functools.partial(kernel, tasks, ndp, chunks),
            out_shape=jax.ShapeDtypeStruct((inputs.shape[1], width), jnp.bfloat16),
            in_specs=[smem, smem, whole, whole],
            out_specs=whole,
            scratch_shapes=scratch,
            compiler_params=pltpu.CompilerParams(collective_id=0, has_side_effects=True,
                                                 vmem_limit_bytes=60 * 1024 * 1024),
        )(task_order, conflict_flags, inputs, cot)

    return jax.shard_map(
        on_device, mesh=mesh,
        in_specs=(P("dp", None), P("task", "dp", None), P(), P()),
        out_specs=P(None, "task"), check_vma=False,
    )
```

time: 475 us -> 183 us (0.39)
  waiting for transfers between devices: 354 us -> 0 us
  Pallas kernels: 0 us -> 178 us
  matrix products: 43.3 us -> 0 us
  blocking collectives: 38.6 us -> 0 us
  local copies, waits for them, and re-layouts: 18.1 us -> 3.05 us
  between operations: 13.5 us -> 0.01 us
  starting transfers between devices: 4.8 us -> 0 us
    reduce_scatter x1 -> x0, waiting for transfers between devices: 282 us -> none  [on_device(): lax.psum_scatter(lax.dot_general(inputs, task_cot, (((0,), (0,)), ((), ()...]
    pallas_call x0 -> x1, Pallas kernels: none -> 178 us  [on_device(): pl.pallas_call(functools.partial(kernel, tasks, ndp, chunks), out_shape=j...]
    all_gather x1 -> x0, waiting for transfers between devices: 49.9 us -> none  [on_device(): lax.all_gather(own_block.astype(jnp.bfloat16), 'dp', axis=0, tiled=True)]
    dot_general x15 -> x0, matrix products: 43.3 us -> none  [the longest x1 14.6 us: on_device(): lax.dot_general(inputs, task_cot, (((0,), (0,)), ((), ())), preferred_ele...]
    psum x1 -> x0, blocking collectives: 38.6 us -> none  [on_device(): gram_matrix = lax.psum(gram_part, ('task', 'dp'))]
    all_to_all x1 -> x0, waiting for transfers between devices: 21.5 us -> none  [on_device(): lax.all_to_all(shard_grad[None], 'task', split_axis=2, concat_axis=0, til...]
    broadcast_in_dim x1 -> x0, local copies, waits for them, and re-layouts: 6.03 us -> none  [on_device(): shard_grad[None]]
  transfers between devices with their start and end apart: 3 -> 0, of which waited for: 3 -> 0; matrix products, arithmetic and copies ran while one was open for 1% -> 0% of each run, Pallas kernels for 0% -> 0%
where the time goes in v1:
time: 183 us; the launch traced here: 181 us
  Pallas kernels  178 us (97%)
  local copies, waits for them, and re-layouts  3.05 us (2%)
    pallas_call x1, Pallas kernels, on_device(): pl.pallas_call(functools.partial(kernel, tasks, ndp, chunks), out_shape=j...  178 us

profile of v1, /device:TPU:0, one launch (start us, length us, event | category | flops | bytes accessed | tf_op | source)
XLA Modules:
  0.0 180.7 jit_solution(3074590290201183650)
XLA Ops:
  0.0 177.7 %shard_map.46 = bf16[4096,256]{1,0:T(8,128)(2,1)} custom-call(s32[4]{0:T(128)} %order_ref.1, s32[4,4]{1,0:T(4,128)} %flags_ref.1, bf16[1024,4096]{1,0:T(8,128)(2,1)} %x_ref.1, bf16[1024,1024]{1,0:T(8,128)(2,1)} %bitcast.1), custom_call_target="tpu_custom_call" | custom-call | tf_op jit(solution)/shard_map/pallas_call | solution.py:213
  177.7 3.0 %copy.6 = bf16[4096,256]{1,0:T(8,128)(2,1)} copy(bf16[4096,256]{1,0:T(8,128)(2,1)} %shard_map.46) | data formatting | bytes 4194304

commit v2 on v1

--- a/solution.py
+++ b/solution.py
@@ -21,8 +21,8 @@
     return code.astype(jnp.int32).astype(jnp.float32) * scale
 
 
-def kernel(tasks, ndp, chunks, order_ref, flags_ref, x_ref, c_ref, out_ref,
-           ysend, yscale, yrecv, yrscale, zsend, zscale, zrecv, zrscale, own,
+def kernel(tasks, ndp, chunks, halves, order_ref, flags_ref, x_ref, c_ref, out_ref,
+           ysend, yscale, yrecv, yrscale, zsend, zscale, zrecv, zrscale, own, cots,
            gsend, grads, gram_own, gram_dp, gram_mid, gram_task,
            ys_sem, yr_sem, zs_sem, zr_sem, ts_sem, tr_sem, gs_sem, gr_sem,
            hs_sem, hr_sem, as_sem, ar_sem):
@@ -32,8 +32,9 @@
     z = me_d // 2
     y = me_d % 2
     rows = x_ref.shape[1] // ndp
-    step = rows // chunks
+    step = rows * halves // chunks
     width = c_ref.shape[1] // tasks
+    part = width // halves
 
     def zof(k):
         return lax.rem(z + k, nz)
@@ -57,9 +58,13 @@
         return copy
 
     def product(zi, yi, c):
-        first = pl.multiple_of(dp_at(zi, yi) * rows + c * step, step)
-        return lax.dot_general(x_ref[:, pl.ds(first, step)], c_ref[...], (((0,), (0,)), ((), ())),
+        first = pl.multiple_of(dp_at(zi, yi) * rows + c // halves * step, step)
+        return lax.dot_general(x_ref[:, pl.ds(first, step)], cots[c % halves], (((0,), (0,)), ((), ())),
                                preferred_element_type=jnp.float32)
+
+    for h in range(halves):
+        for t in range(tasks):
+            cots[h, :, t * part:(t + 1) * part] = c_ref[:, t * width + h * part:t * width + (h + 1) * part]
 
     ycopies, zcopies, tcopies = {}, {}, {}
     for c in range(chunks):
@@ -95,7 +100,7 @@
         for k in range(1, nz):
             total = total + decoded(zrecv[c, k], zrscale[c, k])
         for t in range(tasks):
-            gsend[c, t] = total[:, t * width:(t + 1) * width]
+            gsend[c, t] = total[:, t * part:(t + 1) * part]
         grads[me_t, c] = gsend[c, me_t]
         tcopies[c] = []
         for k in range(1, tasks):
@@ -103,27 +108,32 @@
             tcopies[c].append(send(gsend.at[c, peer], grads.at[me_t, c], ts_sem.at[c, k], tr_sem.at[c, k],
                                    (peer, me_d)))
 
-    second(0)
-    for c in range(1, chunks):
-        second(c)
-        third(c - 1)
-    third(chunks - 1)
+    pairs = [(s, t) for s in range(tasks) for t in range(s, tasks)]
+    sums = {pair: jnp.zeros((8, part), jnp.float32) for pair in pairs}
+
+    def fourth(c):
+        for copy in tcopies[c]:
+            copy.wait_recv()
+        held = [grads[t, c] for t in range(tasks)]
+        for s, t in pairs:
+            both = held[s] * held[t]
+            sums[s, t] = sums[s, t] + jnp.sum(both.reshape(step // 8, 8, part), axis=0)
+
+    for c in range(chunks + 2):
+        if c < chunks:
+            second(c)
+        if 0 <= c - 1 < chunks:
+            third(c - 1)
+        if c >= 2:
+            fourth(c - 2)
 
     line = lax.broadcasted_iota(jnp.int32, (8, 128), 0)
     lane = lax.broadcasted_iota(jnp.int32, (8, 128), 1)
     gram = jnp.zeros((8, 128), jnp.float32)
-    for c in range(chunks):
-        for copy in tcopies[c]:
-            copy.wait_recv()
-    for s in range(tasks):
-        for t in range(s, tasks):
-            def add(c, total, s=s, t=t):
-                both = grads[s, c] * grads[t, c]
-                return total + jnp.sum(both.reshape(step // 8, 8, width), axis=0)
-            total = lax.fori_loop(0, chunks, add, jnp.zeros((8, width), jnp.float32))
-            value = jnp.sum(jnp.sum(total, axis=0, keepdims=True), axis=1, keepdims=True)
-            here = ((line == s) & (lane == t)) | ((line == t) & (lane == s))
-            gram = gram + jnp.where(here, value, 0.0)
+    for s, t in pairs:
+        value = jnp.sum(jnp.sum(sums[s, t], axis=0, keepdims=True), axis=1, keepdims=True)
+        here = ((line == s) & (lane == t)) | ((line == t) & (lane == s))
+        gram = gram + jnp.where(here, value, 0.0)
 
     def swap(value, buffer_own, buffer, count, s_sem, r_sem, device):
         buffer_own[...] = value
@@ -164,7 +174,9 @@
 
     for c in range(chunks):
         mixed = sum(weights[t] * grads[t, c] for t in range(tasks))
-        out_ref[pl.ds(pl.multiple_of(me_d * rows + c * step, step), step), :] = mixed.astype(jnp.bfloat16)
+        first = pl.multiple_of(me_d * rows + c // halves * step, step)
+        h = c % halves
+        out_ref[pl.ds(first, step), h * part:(h + 1) * part] = mixed.astype(jnp.bfloat16)
     mine = block(me_d)
     along = {k: send(mine, mine, as_sem.at[0, k], ar_sem.at[0, k], (me_t, dp_at(zof(k), y)))
              for k in range(1, nz)}
@@ -191,9 +203,11 @@
         cot = cotangent[0]
         rows = inputs.shape[1] // ndp
         step = min(rows, 128)
-        chunks = rows // step
-        kvw = cot.shape[1]
-        width = kvw // tasks
+        width = cot.shape[1] // tasks
+        halves = 2 if width % 256 == 0 else 1
+        chunks = rows // step * halves
+        part = width // halves
+        kvw = part * tasks
         vmem, dma = pltpu.VMEM, pltpu.SemaphoreType.DMA
         f32, i16 = jnp.float32, jnp.int16
         scratch = [
@@ -201,8 +215,8 @@
             vmem((chunks, nz, step, kvw), i16), vmem((chunks, nz, 1, kvw), f32),
             vmem((chunks, nz, step, kvw), i16), vmem((chunks, nz, 1, kvw), f32),
             vmem((chunks, nz, step, kvw), i16), vmem((chunks, nz, 1, kvw), f32),
-            vmem((chunks, step, kvw), f32),
-            vmem((chunks, tasks, step, width), f32), vmem((tasks, chunks, step, width), f32),
+            vmem((chunks, step, kvw), f32), vmem((halves, cot.shape[0], kvw), cot.dtype),
+            vmem((chunks, tasks, step, part), f32), vmem((tasks, chunks, step, part), f32),
             vmem((8, 128), f32), vmem((ndp, 8, 128), f32), vmem((8, 128), f32), vmem((tasks, 8, 128), f32),
             dma((chunks, 2)), dma((chunks, 2)), dma((chunks, nz, 2)), dma((chunks, nz, 2)),
             dma((chunks, tasks)), dma((chunks, tasks)), dma((ndp,)), dma((ndp,)),
@@ -211,7 +225,7 @@
         smem = pl.BlockSpec(memory_space=pltpu.SMEM)
         whole = pl.BlockSpec(memory_space=pltpu.VMEM)
         return pl.pallas_call(
-            functools.partial(kernel, tasks, ndp, chunks),
+            functools.partial(kernel, tasks, ndp, chunks, halves),
             out_shape=jax.ShapeDtypeStruct((inputs.shape[1], width), jnp.bfloat16),
             in_specs=[smem, smem, whole, whole],
             out_specs=whole,

time: 183 us -> 169 us (0.923)
  Pallas kernels: 178 us -> 163 us
    pallas_call x1, Pallas kernels: 178 us -> 163 us  [on_device(): pl.pallas_call(functools.partial(kernel, tasks, ndp, chunks, halves), out...]
where the time goes in v2:
time: 169 us; the launch traced here: 167 us
  Pallas kernels  163 us (96%)
  local copies, waits for them, and re-layouts  3.05 us (2%)
    pallas_call x1, Pallas kernels, on_device(): pl.pallas_call(functools.partial(kernel, tasks, ndp, chunks, halves), out...  163 us

profile of v2, /device:TPU:0, one launch (start us, length us, event | category | flops | bytes accessed | tf_op | source)
XLA Modules:
  0.0 166.5 jit_solution(10309919518672502743)
XLA Ops:
  0.0 163.5 %shard_map.46 = bf16[4096,256]{1,0:T(8,128)(2,1)} custom-call(s32[4]{0:T(128)} %order_ref.1, s32[4,4]{1,0:T(4,128)} %flags_ref.1, bf16[1024,4096]{1,0:T(8,128)(2,1)} %x_ref.1, bf16[1024,1024]{1,0:T(8,128)(2,1)} %bitcast.1), custom_call_target="tpu_custom_call" | custom-call | tf_op jit(solution)/shard_map/pallas_call | solution.py:227
  163.5 3.0 %copy.6 = bf16[4096,256]{1,0:T(8,128)(2,1)} copy(bf16[4096,256]{1,0:T(8,128)(2,1)} %shard_map.46) | data formatting | bytes 4194304
